TPU v7x, 256 devices: a whole 4x4x8 slice. The times are simulated.
256 devices in a mesh: band: 64 (over z, y_hi, x), ga: 4 (over y_lo, core).
Axes of the slice: x: 4, y: 4 (y_hi: 2, y_lo: 2; y = y_hi * 2 + y_lo), z: 8, core: 2. Of those that a mesh axis runs over, the one named last changes fastest.
Arguments:
- elements: bfloat16 [2, 6144, 2048], P(None, 'band', 'ga'), may hold values from -0.75 to 0.75
- screened: bfloat16 [2, 2, 2048, 2048], P(None, None, 'ga'), may hold values from -0.09375 to 0.09375
- energies: float32 [6144], replicated, may hold values from -3 to 3
- freq_points: float32 [2], replicated, may hold values from -3 to 3
- freq_weights: float32 [2], replicated, may hold values from 0.5 to 2
- band_of_slot: int32 [6144], replicated, may hold values from 0 to 6143, each once
Outputs:
- sigma: float32 [2, 6144, 6144], P(None, 'band', 'ga')
Inputs may be any that keep to these rules, and one draw needn't show every extreme that they name: `band_of_slot`: each of 0 to 6143 stands once.
All inputs are finite; a program needn't handle non-finite values.
Results may differ from a plain program's by a relative error of at most 0.0042.
Values may be sent and summed in bfloat16 or wider, within the bound.
A program may use at most 128 MiB of HBM per device.

v0:
```python
import jax
import jax.numpy as jnp
from jax import lax
from jax.sharding import Mesh
from jax.sharding import PartitionSpec as P

GA = ("ga_0", "ga_1")


def in_order(blocks, dim):
    shape = list(blocks.shape[1:])
    shape[dim] *= blocks.shape[0]
    return jnp.moveaxis(blocks, 0, dim).reshape(shape)


def all_blocks(shard, axes, order):
    blocks = shard
    for k in order:
        blocks = lax.all_gather(blocks, axes[k])
    done = order[::-1]
    back = [done.index(k) for k in range(len(axes))]
    blocks = blocks.transpose(*back, *range(len(axes), blocks.ndim))
    return blocks.reshape(-1, *shard.shape)


def gathered_by_axis(shard, axes, order, dim):
    return in_order(all_blocks(shard, axes, order), dim)


def split_up(shard, dim, peers):
    shape = shard.shape
    blocks = shard.reshape(*shape[:dim], peers, shape[dim] // peers, *shape[dim + 1 :])
    return jnp.moveaxis(blocks, dim, 0)


def summed_on_arrival(shard, axis, dim):
    blocks = split_up(shard, dim, lax.axis_size(axis))
    arrived = lax.all_to_all(blocks, axis, split_axis=0, concat_axis=0, tiled=True)
    return arrived.astype(jnp.float32).sum(axis=0)


def make_left(block):
    flipped = jnp.stack([-block[1], block[0]])
    return jnp.stack([block, flipped])


def on_device(elements, screened, energies, freq_points, freq_weights, band_of_slot):
    bands = elements.shape[1]
    slot_energy = jnp.take(energies, band_of_slot)
    offset = slot_energy[None, :] - freq_points[:, None]
    screen = freq_weights[:, None] / (1.0 + 4.0 * offset * offset)
    own_start = lax.axis_index("band") * bands
    screen_own = lax.dynamic_slice_in_dim(screen, own_start, bands, 1)
    piece = gathered_by_axis(elements, GA, (0, 1), 2)
    real_side = jnp.stack([piece[0], -piece[1]])
    imag_side = jnp.stack([piece[1], piece[0]])
    sides = jnp.stack([real_side, imag_side])
    applied = jnp.einsum(
        "dcmk,wcgk->wdmg", sides, screened, preferred_element_type=jnp.float32
    ).astype(jnp.bfloat16)
    left_own = make_left(elements)
    pairs = jnp.einsum(
        "dcnk,wcmk->wdnm",
        left_own,
        lax.all_gather(applied, "band", axis=2, tiled=True),
        preferred_element_type=jnp.float32,
    )
    factor = 0.5 * (screen_own[:, :, None] + screen[:, None, :])
    partial_rows = jnp.sum(pairs * factor[:, None], axis=0)
    return summed_on_arrival(partial_rows.astype(jnp.bfloat16), GA, 2)


def solution(mesh):
    torus = Mesh(mesh.devices.reshape(mesh.shape["band"], 2, 2), ("band", "ga_0", "ga_1"))
    return jax.shard_map(
        on_device,
        mesh=torus,
        in_specs=(P(None, "band", GA), P(None, None, GA, None), P(), P(), P(), P()),
        out_specs=P(None, "band", GA),
        check_vma=False,
    )
```

profile of v0, /device:TPU:1, one launch (start us, length us, event | category | flops | bytes accessed | tf_op | source)
XLA Modules:
  0.0 343.5 jit_solution(7880529084560656010)
XLA Ops:
  6.5 0.0 copy-start
  6.5 6.5 %all-gather = bf16[4,96,512]{2,1,0:T(8,128)(2,1)S(1)} all-gather(bf16[2,96,512]{2,1,0:T(8,128)(2,1)} %param.6), channel_id=2, replica_groups=mesh['band'=64,'ga_0'=2,'ga_1'=2] {'ga_0'}, dimensions={0}, use_global_device_ids=true | all-gather | bytes 589824 | tf_op jit(solution)/shard_map/all_gather | solution.py:19
  13.0 5.5 %all-gather.1 = bf16[4,2,96,512]{3,2,1,0:T(8,128)(2,1)S(1)} all-gather(bf16[2,2,96,512]{3,2,1,0:T(8,128)(2,1)S(1)} %bitcast.72), channel_id=3, replica_groups=mesh['band'=64,'ga_0'=2,'ga_1'=2] {'ga_1'}, dimensions={0}, use_global_device_ids=true | all-gather | bytes 1179648 | tf_op jit(solution)/shard_map/all_gather | solution.py:19
  18.5 0.1 copy.15
  18.6 0.1 slice_bitcast_fusion
  18.7 0.1 neg.14
  18.8 0.1 maximum_bitcast_fusion.8
  19.0 0.0 copy-start.2
  19.0 3.7 %fusion.15 = bf16[2,2,96,512]{3,2,1,0:T(8,128)(2,1)} fusion(bf16[2,2,512,2048]{3,2,1,0:T(8,128)(2,1)S(1)} %copy-done.5, bf16[1,2,96,2048]{3,2,1,0:T(8,128)(2,1)S(1)} %get-tuple-element.8, bf16[1,2,96,2048]{3,2,1,0:T(8,128)(2,1)S(1)} %get-tuple-element.7), kind=kOutput, calls=%fused_computation.14 | convolution fusion | flops 1613955072 | bytes 10354688 | tf_op jit(solution)/shard_map/dcmk,wcgk->wdmg/dot_general | solution.py:58
  22.6 0.0 all-gather.4.cloned.1.call-update
  22.7 0.0 copy-start.3
  22.7 0.0 copy-start.4
  22.7 0.0 copy-start.1
  22.7 34.3 %gather_fusion = f32[6144]{0:T(1024)S(1)} fusion(f32[6144]{0:T(1024)S(1)} %copy-done, s32[6144]{0:T(1024)S(1)} %fusion.22), kind=kCustom, calls=%fused_computation | custom fusion | bytes 73728 | tf_op jit(solution)/shard_map/jit(_take)/gather | solution.py:49
  57.1 0.1 fusion.21
  57.2 0.1 constant_dynamic-slice_fusion
  57.3 0.0 copy-done.1
  57.3 2.7 add_multiply_fusion
  60.0 223.9 %all-gather.4.cloned.1.call-done = bf16[2,2,6144,512]{3,2,1,0:T(8,128)(2,1)} async-done(((bf16[2,2,96,512]{3,2,1,0:T(8,128)(2,1)}), bf16[2,2,6144,512]{3,2,1,0:T(8,128)(2,1)}) %all-gather.4.cloned.1.call-update) | async-done | bytes 25165840 | tf_op jit(solution)/shard_map/all_gather | solution.py:65
  284.0 16.0 %fusion.2 = bf16[2,96,6144]{2,1,0:T(8,128)(2,1)} fusion(bf16[2,2,6144,512]{3,2,1,0:T(8,128)(2,1)} %all-gather.4.cloned.1.call-done, f32[2,96,6144]{2,1,0:T(8,128)} %add_multiply_fusion, bf16[1,2,96,512]{3,2,1,0:T(8,128)(2,1)S(1)} %maximum_bitcast_fusion.12, bf16[1,2,96,512]{3,2,1,0:T(8,128)(2,1)S(1)} %bitcast.74), kind=kOutput, calls=%fused_computation.4 | convolution fusion | flops 4836163584 | bytes 32636928 | tf_op jit(solution)/shard_map/dcnk,wcmk->wdnm/dot_general | solution.py:62
  300.0 3.5 %convert_element_type.19 = bf16[2,96,4,1536]{3,2,1,0:T(4,128)(2,1)S(1)} reshape(bf16[2,96,6144]{2,1,0:T(8,128)(2,1)} %fusion.2) | data formatting | bytes 4718592 | tf_op jit(solution)/shard_map/convert_element_type | solution.py:70
  303.5 0.4 copy.18
  303.9 31.3 %all_to_all.5 = bf16[4,2,96,1536]{3,2,1,0:T(8,128)(2,1)S(1)} all-to-all(bf16[4,2,96,1536]{3,2,1,0:T(8,128)(2,1)S(1)} %copy.18), channel_id=1, replica_groups=mesh['band'=64,'ga_0'=2,'ga_1'=2] {'ga_0','ga_1'}, dimensions={0} | all-to-all | bytes 4718592 | tf_op jit(solution)/shard_map/all_to_all | solution.py:38
  335.2 1.4 convert_reduce_fusion
  (13 shorter events, 0.1 us)
Async XLA Ops:
  6.5 16.2 %copy-start = (f32[6144]{0:T(1024)S(1)}, f32[6144]{0:T(1024)}, u32[]{:S(2)}) copy-start(f32[6144]{0:T(1024)} %param.8) | copy-start | bytes 73732
  6.5 277.5 %all-gather.4.cloned.1.call-start = ((), (), s32[]{:S(2)}) async-start(), calls=%async_computation.1 | async-start | bytes 25559040 | tf_op jit(solution)/shard_map/all_gather | solution.py:65
  13.0 5.9 %copy-start.5 = (bf16[2,2,512,2048]{3,2,1,0:T(8,128)(2,1)S(1)}, bf16[2,2,512,2048]{3,2,1,0:T(8,128)(2,1)}, u32[]{:S(2)}) copy-start(bf16[2,2,512,2048]{3,2,1,0:T(8,128)(2,1)} %param.7) | copy-start | bytes 25165828
  19.0 3.7 %copy-start.2 = (s32[6144]{0:T(1024)S(1)}, s32[6144]{0:T(1024)}, u32[]{:S(2)}) copy-start(s32[6144]{0:T(1024)} %param.11) | copy-start | bytes 73732
  22.7 34.3 %copy-start.3 = (f32[2]{0:T(128)S(1)}, f32[2]{0:T(128)}, u32[]{:S(2)}) copy-start(f32[2]{0:T(128)} %param.10) | copy-start | bytes 28
  22.7 34.3 %copy-start.4 = (f32[2]{0:T(128)S(1)}, f32[2]{0:T(128)}, u32[]{:S(2)}) copy-start(f32[2]{0:T(128)} %param.9) | copy-start | bytes 28
  22.7 34.5 %copy-start.1 = (bf16[2,96,512]{2,1,0:T(8,128)(2,1)S(1)}, bf16[2,96,512]{2,1,0:T(8,128)(2,1)}, u32[]{:S(2)}) copy-start(bf16[2,96,512]{2,1,0:T(8,128)(2,1)} %param.6) | copy-start | bytes 589828
Sparse Core Ops, SparseCore 0:
  22.8 261.1 all-gather.3
where the time goes:
time: 344 us; the launch traced here: 343 us
  waiting for transfers between devices  224 us (65%)
  blocking collectives  43.3 us (13%)
  local copies, waits for them, and re-layouts  38.5 us (11%)
  matrix products  19.6 us (6%)
  between operations  13.6 us (4%)
  other arithmetic  4.5 us (1%)
    all_gather x1, waiting for transfers between devices, on_device(): lax.all_gather(applied, 'band', axis=2, tiled=True)  224 us
    gather x1, local copies, waits for them, and re-layouts, on_device(): slot_energy = jnp.take(energies, band_of_slot)  34.3 us
    all_to_all x1, blocking collectives, summed_on_arrival(): lax.all_to_all(blocks, axis, split_axis=0, concat_axis=0, tiled=True)  31.3 us
    dot_general x1, matrix products, on_device(): jnp.einsum('dcnk,wcmk->wdnm', left_own, lax.all_gather(applied, 'band', a...  16 us
    all_gather x2, blocking collectives, all_blocks(): blocks = lax.all_gather(blocks, axes[k])  12 us
  transfers between devices with their start and end apart: 1, of which 1 were waited for; matrix products, arithmetic and copies ran while one was open for 11% of the time, Pallas kernels for 0%

commit v1 on v0

--- a/solution.py
+++ b/solution.py
@@ -59,10 +59,16 @@
         "dcmk,wcgk->wdmg", sides, screened, preferred_element_type=jnp.float32
     ).astype(jnp.bfloat16)
     left_own = make_left(elements)
+    paths_number = lambda field, which_axis: jnp.concatenate(
+        jax.lax.all_to_all(
+            jnp.stack([field for _ in range(jax.lax.axis_size(which_axis))]), which_axis, 0, 0
+        ),
+        axis=2,
+    )
     pairs = jnp.einsum(
         "dcnk,wcmk->wdnm",
         left_own,
-        lax.all_gather(applied, "band", axis=2, tiled=True),
+        paths_number(applied, "band"),
         preferred_element_type=jnp.float32,
     )
     factor = 0.5 * (screen_own[:, :, None] + screen[:, None, :])

time: 344 us -> 742 us (2.16)
  the two profiles are of different devices: /device:TPU:1 before, /device:TPU:100 now
where the time goes in v1:
time: 742 us
  waiting for transfers between devices  590 us (80%)
  local copies, waits for them, and re-layouts  70.5 us (10%)
  blocking collectives  41 us (6%)
  matrix products  21.6 us (3%)
  starting transfers between devices  13.6 us (2%)
    all_to_all x1, waiting for transfers between devices, on_device(): jax.lax.all_to_all(jnp.stack([field for _ in range(jax.lax.axis_size(whic...  590 us
    gather x1, local copies, waits for them, and re-layouts, on_device(): slot_energy = jnp.take(energies, band_of_slot)  34.3 us
    all_to_all x1, blocking collectives, summed_on_arrival(): lax.all_to_all(blocks, axis, split_axis=0, concat_axis=0, tiled=True)  31 us
    reshape x1, local copies, waits for them, and re-layouts, on_device(): jnp.concatenate(jax.lax.all_to_all(jnp.stack([field for _ in range(jax.la...  21.4 us
    dot_general x1, matrix products, on_device(): jnp.einsum('dcnk,wcmk->wdnm', left_own, paths_number(applied, 'band'), pr...  15.3 us
  transfers between devices with their start and end apart: 1, of which 1 were waited for; matrix products, arithmetic and copies ran while one was open for 5% of the time, Pallas kernels for 0%

profile of v1, /device:TPU:100, one launch (start us, length us, event | category | flops | bytes accessed | tf_op | source)
XLA Modules:
  0.0 741.6 jit_solution(6393979669843392349)
XLA Ops:
  0.0 7.6 %all-gather = bf16[4,96,512]{2,1,0:T(8,128)(2,1)S(1)} all-gather(bf16[2,96,512]{2,1,0:T(8,128)(2,1)} %param.6), channel_id=2, replica_groups=mesh['band'=64,'ga_0'=2,'ga_1'=2] {'ga_0'}, dimensions={0}, use_global_device_ids=true | all-gather | bytes 589824 | tf_op jit(solution)/shard_map/all_gather | solution.py:19
  7.6 2.4 all-gather.1
  10.0 0.8 copy.14
  10.8 0.3 reshape.76
  11.1 0.3 fusion.21
  11.4 0.3 squeeze.4
  11.7 0.1 neg.14
  11.8 0.3 slice.19
  12.0 0.1 maximum_bitcast_fusion.8
  12.2 6.3 fusion.11
  18.5 8.7 %stack.23 = bf16[64,2,2,96,512]{4,3,2,1,0:T(8,128)(2,1)} broadcast(bf16[2,2,96,512]{3,2,1,0:T(8,128)(2,1)S(1)} %copy.15), dimensions={1,2,3,4} | broadcast | bytes 25559040 | tf_op jit(solution)/shard_map/stack | solution.py:64
  27.3 13.6 %all-to-all-start = ((bf16[64,2,2,96,512]{4,3,2,1,0:T(8,128)(2,1)}), bf16[64,2,2,96,512]{4,3,2,1,0:T(8,128)(2,1)}, u32[]{:S(2)}, u32[]{:S(2)}) async-start(bf16[64,2,2,96,512]{4,3,2,1,0:T(8,128)(2,1)} %stack.23), calls=%async_computation | async-start | bytes 50331648 | tf_op jit(solution)/shard_map/all_to_all | solution.py:63
  40.9 0.0 copy-start.5
  41.0 34.3 %gather_fusion = f32[6144]{0:T(1024)S(1)} fusion(f32[6144]{0:T(1024)S(1)} %copy-done, s32[6144]{0:T(1024)S(1)} %fusion.18), kind=kCustom, calls=%fused_computation | custom fusion | bytes 73728 | tf_op jit(solution)/shard_map/jit(_take)/gather | solution.py:49
  75.3 0.1 fusion.17
  75.4 0.1 constant_dynamic-slice_fusion
  75.5 2.8 add_multiply_fusion
  78.3 590.2 %all-to-all-done = bf16[64,2,2,96,512]{4,3,2,1,0:T(8,128)(2,1)} async-done(((bf16[64,2,2,96,512]{4,3,2,1,0:T(8,128)(2,1)}), bf16[64,2,2,96,512]{4,3,2,1,0:T(8,128)(2,1)}, u32[]{:S(2)}, u32[]{:S(2)}) %all-to-all-start) | async-done | bytes 25165856 | tf_op jit(solution)/shard_map/all_to_all | solution.py:63
  668.5 21.4 %copy.16 = bf16[2,2,64,96,512]{4,3,2,1,0:T(8,128)(2,1)} copy(bf16[2,2,64,96,512]{4,3,1,0,2:T(8,128)(2,1)} %bitcast.12) | data formatting | bytes 50331648 | tf_op jit(solution)/shard_map/reshape | solution.py:62
  690.0 15.3 %fusion = bf16[2,96,6144]{2,1,0:T(8,128)(2,1)} fusion(bf16[2,2,6144,512,1]{3,2,1,4,0:T(8,128)(2,1)} %bitcast.61, f32[2,96,6144]{2,1,0:T(8,128)S(1)} %copy-done.2, bf16[1,2,96,512]{3,2,1,0:T(8,128)(2,1)S(1)} %maximum_bitcast_fusion.12, bf16[1,2,96,512]{3,2,1,0:T(8,128)(2,1)S(1)} %bitcast.66), kind=kOutput, calls=%fused_computation.2 | convolution fusion | flops 4836163584 | bytes 32636928 | tf_op jit(solution)/shard_map/dcnk,wcmk->wdnm/dot_general | solution.py:68
  705.3 3.5 convert_element_type.19
  708.8 0.4 copy.17
  709.3 31.0 %all_to_all.10 = bf16[4,2,96,1536]{3,2,1,0:T(8,128)(2,1)S(1)} all-to-all(bf16[4,2,96,1536]{3,2,1,0:T(8,128)(2,1)S(1)} %copy.17), channel_id=1, replica_groups=mesh['band'=64,'ga_0'=2,'ga_1'=2] {'ga_0','ga_1'}, dimensions={0} | all-to-all | bytes 4718592 | tf_op jit(solution)/shard_map/all_to_all | solution.py:38
  740.2 1.4 convert_reduce_fusion
  (18 shorter events, 0.1 us)
Async XLA Ops:
  0.0 40.9 %copy-start = (f32[6144]{0:T(1024)S(1)}, f32[6144]{0:T(1024)}, u32[]{:S(2)}) copy-start(f32[6144]{0:T(1024)} %param.8) | copy-start | bytes 73732
  27.3 13.6 %copy-start.4 = (s32[6144]{0:T(1024)S(1)}, s32[6144]{0:T(1024)}, u32[]{:S(2)}) copy-start(s32[6144]{0:T(1024)} %param.11) | copy-start | bytes 73732
  27.3 641.2 %all-to-all-start = ((bf16[64,2,2,96,512]{4,3,2,1,0:T(8,128)(2,1)}), bf16[64,2,2,96,512]{4,3,2,1,0:T(8,128)(2,1)}, u32[]{:S(2)}, u32[]{:S(2)}) async-start(bf16[64,2,2,96,512]{4,3,2,1,0:T(8,128)(2,1)} %stack.23), calls=%async_computation | async-start | bytes 50331648 | tf_op jit(solution)/shard_map/all_to_all | solution.py:63
  40.9 34.3 %copy-start.5 = (f32[2]{0:T(128)S(1)}, f32[2]{0:T(128)}, u32[]{:S(2)}) copy-start(f32[2]{0:T(128)} %param.10) | copy-start | bytes 28
  40.9 34.3 %copy-start.6 = (f32[2]{0:T(128)S(1)}, f32[2]{0:T(128)}, u32[]{:S(2)}) copy-start(f32[2]{0:T(128)} %param.9) | copy-start | bytes 28
  40.9 34.5 %copy-start.3 = (bf16[2,96,512]{2,1,0:T(8,128)(2,1)S(1)}, bf16[2,96,512]{2,1,0:T(8,128)(2,1)}, u32[]{:S(2)}) copy-start(bf16[2,96,512]{2,1,0:T(8,128)(2,1)} %param.6) | copy-start | bytes 589828
  668.5 21.4 %copy-start.2 = (f32[2,96,6144]{2,1,0:T(8,128)S(1)}, f32[2,96,6144]{2,1,0:T(8,128)}, u32[]{:S(2)}) copy-start(f32[2,96,6144]{2,1,0:T(8,128)} %add_multiply_fusion) | copy-start | bytes 14155780
  708.8 32.8 %copy-start.1 = (f32[6144]{0:T(1024)S(1)}, f32[6144]{0:T(1024)}, u32[]{:S(2)}) copy-start(f32[6144]{0:T(1024)} %param.8) | copy-start | bytes 73732
